TPU v7x, 32 devices: a whole 2x2x4 slice. The times are simulated.
32 devices in a mesh: rows: 32 (over z, y, x, core).
Axes of the slice: x: 2, y: 2, z: 4, core: 2. Of those that a mesh axis runs over, the one named last changes fastest.
Arguments:
- adj_diag: int32 [512, 512], P('rows'), may hold values from -2147483648 to 2147483647
- adj_right: int32 [512, 512], P('rows'), may hold values from -2147483648 to 2147483647
- alive_diag: int32 [512, 512], P('rows'), may hold values from -2147483648 to 2147483647
- alive_right: int32 [512, 512], P('rows'), may hold values from -2147483648 to 2147483647
- truss_k: int32 [1], replicated, may hold values from 130 to 193
Outputs:
- support_field: float32 [16384, 1024], P('rows')
- removed_counts: int32 [3], replicated
All inputs are finite; a program needn't handle non-finite values.
Results may differ from a plain program's by a relative error of at most 0.0003.
Values may be sent and summed in bfloat16 or wider, within the bound.
A program may use at most 64 MiB of HBM per device.

v0:
```python
import jax
import jax.numpy as jnp
from jax import lax
from jax.sharding import PartitionSpec as P

ITERS = 3


def shifted(array, axis, by):
    count = lax.axis_size(axis)
    return lax.ppermute(array, axis, [(i, (i + by) % count) for i in range(count)])


def unpack_tile(packed):
    shifts = jnp.arange(32, dtype=jnp.int32)
    tile_bits = packed[:, None, :] >> shifts[None, :, None] & 1
    return tile_bits.reshape(packed.shape[0] * 32, packed.shape[1])


def pack_bits(tile_bits):
    shifts = jnp.arange(32, dtype=jnp.int32)
    sectioned = tile_bits.reshape(tile_bits.shape[0] // 32, 32, tile_bits.shape[1])
    return jnp.sum(sectioned << shifts[None, :, None], axis=1, dtype=jnp.int32)


def within_tile(packed):
    upper_half = jnp.triu(unpack_tile(packed), 1)
    return (upper_half + upper_half.T).astype(jnp.bfloat16)


def across_tile(packed):
    return unpack_tile(packed).astype(jnp.bfloat16)


def pack_across(across):
    return pack_bits(across.astype(jnp.int32))


def fold_within(within):
    width = within.shape[0]
    half = width // 2
    row_ids = lax.broadcasted_iota(jnp.int32, (half, width), 0)
    col_ids = lax.broadcasted_iota(jnp.int32, (half, width), 1)
    flipped = within[half:][::-1, ::-1]
    folded = jnp.where(col_ids > row_ids, within[:half], flipped)
    return pack_bits(folded.astype(jnp.int32))


def unfold_within(packed):
    folded = unpack_tile(packed)
    half = folded.shape[0]
    width = folded.shape[1]
    row_ids = lax.broadcasted_iota(jnp.int32, (half, width), 0)
    col_ids = lax.broadcasted_iota(jnp.int32, (half, width), 1)
    top_rows = jnp.where(col_ids > row_ids, folded, jnp.zeros_like(folded))
    bottom_rows = jnp.where(col_ids < row_ids, folded, jnp.zeros_like(folded))[::-1, ::-1]
    upper_half = jnp.concatenate([top_rows, bottom_rows], axis=0)
    return (upper_half + upper_half.T).astype(jnp.bfloat16)


def support_within(prev_across, within, across):
    inside = lax.dot_general(
        prev_across, prev_across, (((0,), (0,)), ((), ())), preferred_element_type=jnp.float32
    )
    inside = inside + jnp.dot(within, within, preferred_element_type=jnp.float32)
    return inside + lax.dot_general(
        across, across, (((1,), (1,)), ((), ())), preferred_element_type=jnp.float32
    )


def support_across(within, across, next_within):
    between = jnp.dot(within, across, preferred_element_type=jnp.float32)
    return between + jnp.dot(across, next_within, preferred_element_type=jnp.float32)


def keep_edges(support, tile_mask, thresh):
    return jnp.where(support >= thresh, tile_mask, jnp.zeros_like(tile_mask))


def peel(prev_across, within, across, next_within, thresh):
    inside = support_within(prev_across, within, across)
    between = support_across(within, across, next_within)
    return (
        inside,
        between,
        keep_edges(inside, within, thresh),
        keep_edges(between, across, thresh),
    )


def tally(within, new_within, across, new_across):
    removed = jnp.sum((within - new_within).astype(jnp.int32)) // 2
    removed = removed + jnp.sum((across - new_across).astype(jnp.int32))
    return removed


def on_device(adj_diag, adj_right, alive_diag, alive_right, truss_k):
    within = within_tile(adj_diag & alive_diag)
    across_words = adj_right & alive_right
    across = across_tile(across_words)
    thresh = (truss_k[0] - 2).astype(jnp.float32)
    counts = []
    for step in range(ITERS):
        prev_across = across_tile(shifted(pack_across(across), "rows", 1))
        next_within = unfold_within(shifted(fold_within(within), "rows", -1))
        inside, between, new_within, new_across = peel(
            prev_across, within, across, next_within, thresh
        )
        counts.append(tally(within, new_within, across, new_across))
        within, across = (new_within, new_across)
    stacked = jnp.stack(counts)
    stacked = lax.psum(stacked, "rows")
    support = jnp.concatenate(
        [inside * within.astype(jnp.float32), between * across.astype(jnp.float32)], axis=1
    )
    return (support, stacked)


def solution(mesh):
    in_specs = (P("rows", None), P("rows", None), P("rows", None), P("rows", None), P())
    out_specs = (P("rows", None), P())
    return jax.shard_map(
        on_device, mesh=mesh, in_specs=in_specs, out_specs=out_specs, check_vma=False
    )
```

profile of v0, /device:TPU:12, one launch (start us, length us, event | category | flops | bytes accessed | tf_op | source)
XLA Modules:
  0.0 112.2 jit_solution(5490259086250720770)
XLA Ops:
  0.7 0.8 and.74
  2.4 0.9 rev.18
  3.5 0.9 collective-permute-start.1
  4.9 1.4 %fusion.47 = f32[512,512]{1,0:T(8,128)} fusion(bf16[512,512]{1,0:T(8,128)(2,1)S(1)} %get-tuple-element.17, bf16[512,512]{1,0:T(8,128)(2,1)S(1)} %get-tuple-element.16), kind=kOutput, calls=%fused_computation.93 | convolution fusion | flops 268435456 | bytes 2097152 | tf_op jit(solution)/shard_map/dot_general | solution.py:72
  7.2 0.8 rev.19
  7.9 1.1 pad_add_fusion
  9.0 2.6 %copy.8 = s32[512,512]{0,1:T(8,128)} copy(s32[512,512]{1,0:T(8,128)} %pad_add_fusion) | data formatting | bytes 2097152 | tf_op jit(solution)/shard_map/concatenate | solution.py:57
  11.6 2.2 %fusion.8 = (s32[16,512]{1,0:T(8,128)S(1)}, bf16[512,512]{1,0:T(8,128)(2,1)S(1)}) fusion(bf16[512,512]{1,0:T(8,128)(2,1)S(1)} %get-tuple-element.16, f32[]{:T(128)} %bitcast.4, f32[512,512]{1,0:T(8,128)} %fusion.47, s32[512,512]{0,1:T(8,128)} %copy.8, s32[256,512]{1,0:T(8,128)S(1)} %rev.19, s32[256,512]{1,0:T(8,128)S(1)} %get-tuple-element.14), kind=kOutput, calls=%fused_computation.25 | convolution fusion | flops 270786560 | bytes 4227076 | tf_op jit(solution)/shard_map/dot_general | solution.py:73
  13.8 0.8 collective-permute-start.4
  15.5 0.5 fusion.7
  16.1 0.9 rev.20
  17.1 2.0 %collective-permute-start.2 = (s32[8,512]{1,0:T(8,128)S(1)}, s32[8,512]{1,0:T(8,128)S(1)}, u32[]{:S(2)}, u32[]{:S(2)}) collective-permute-start(s32[8,512]{1,0:T(8,128)S(1)} %fusion.24), channel_id=1, source_target_pairs={{0,31},{1,0},{2,1},{3,2},{4,3},{5,4},{6,5},{7,6},{8,7},{9,8},{10,9... | collective-permute-start | bytes 49160 | tf_op jit(solution)/shard_map/ppermute | solution.py:11
  20.0 0.5 fusion.6
  20.5 0.9 rev.22
  21.6 0.6 collective-permute-start.5
  22.2 1.4 %fusion.48 = f32[512,512]{1,0:T(8,128)} fusion(bf16[512,512]{1,0:T(8,128)(2,1)S(1)} %fusion.7, bf16[512,512]{1,0:T(8,128)(2,1)S(1)} %get-tuple-element.21), kind=kOutput, calls=%fused_computation.94 | convolution fusion | flops 268435456 | bytes 2097152 | tf_op jit(solution)/shard_map/dot_general | solution.py:72
  23.6 1.4 %fusion.28 = (s32[256,512]{1,0:T(8,128)}, s32[256,512]{1,0:T(8,128)}, s32[256,512]{1,0:T(8,128)}, s32[256,512]{1,0:T(8,128)S(1)}) fusion(s32[8,512]{1,0:T(8,128)S(1)} %collective-permute-done.5, s32[256]{0:T(256)S(1)} %shift_left.64, s32[8,512]{1,0:T(8,128)S(1)} %collective-permute-done.2), kind=kLoop, calls=%fused_computation.69 | loop fusion | flops 1310720 | bytes 2130944 | tf_op jit(solution)/shard_map/jit(_where)/select_n | solution.py:55
  25.0 3.9 %rev.21 = s32[256,512]{1,0:T(8,128)S(1)} reverse(s32[256,512]{1,0:T(8,128)} %get-tuple-element.18), dimensions={0,1} | reverse | bytes 1048576 | tf_op jit(solution)/shard_map/rev | solution.py:56
  28.9 1.1 pad_add_fusion.1
  30.0 2.6 %copy.9 = s32[512,512]{0,1:T(8,128)} copy(s32[512,512]{1,0:T(8,128)} %pad_add_fusion.1) | data formatting | bytes 2097152 | tf_op jit(solution)/shard_map/concatenate | solution.py:57
  32.5 2.4 %fusion.9 = (s32[16,512]{1,0:T(8,128)S(1)}, bf16[512,512]{1,0:T(8,128)(2,1)S(1)}) fusion(bf16[512,512]{1,0:T(8,128)(2,1)S(1)} %get-tuple-element.21, f32[]{:T(128)} %bitcast.4, f32[512,512]{1,0:T(8,128)} %fusion.48, s32[512,512]{0,1:T(8,128)} %copy.9, s32[256,512]{1,0:T(8,128)S(1)} %rev.21, s32[256,512]{1,0:T(8,128)} %copy-done.1), kind=kOutput, calls=%fused_computation.27 | convolution fusion | flops 270786560 | bytes 4227076 | tf_op jit(solution)/shard_map/dot_general | solution.py:73
  34.9 1.0 collective-permute-start.3
  36.0 3.8 %rev.23 = s32[256,512]{1,0:T(8,128)S(1)} reverse(s32[256,512]{1,0:T(8,128)} %get-tuple-element.11), dimensions={0,1} | reverse | bytes 1048576 | tf_op jit(solution)/shard_map/rev | solution.py:56
  39.7 2.1 %pad_add_fusion.2 = s32[512,512]{1,0:T(8,128)} fusion(s32[256,512]{1,0:T(8,128)S(1)} %rev.23, s32[256,512]{1,0:T(8,128)} %get-tuple-element.10), kind=kLoop, calls=%fused_computation.23 | loop fusion | flops 262144 | bytes 2097152 | tf_op jit(solution)/shard_map/concatenate | solution.py:57
  41.8 2.5 %copy.13 = s32[512,512]{0,1:T(8,128)} copy(s32[512,512]{1,0:T(8,128)} %pad_add_fusion.2) | data formatting | bytes 2097152 | tf_op jit(solution)/shard_map/concatenate | solution.py:57
  44.8 0.6 copy-done
  45.8 1.5 %convert_multiply_fusion = (f32[512,512]{1,0:T(8,128)}, f32[512,512]{1,0:T(8,128)S(1)}) fusion(bf16[512,512]{1,0:T(8,128)(2,1)S(1)} %get-tuple-element.25, f32[]{:T(128)} %bitcast.4, f32[512,512]{1,0:T(8,128)S(1)} %fusion.49, s32[512,512]{0,1:T(8,128)S(1)} %copy-done.3, s32[256,512]{1,0:T(8,128)S(1)} %rev.23, s32[256,512]{1,0:T(8,128)S(1)} %copy-done), kind=kOutput, calls=%fused_computation.48 | convolution fusion | flops 270532608 | bytes 5767172 | tf_op jit(solution)/shard_map/dot_general | solution.py:73
  47.3 1.5 %convert_reduce_fusion.4 = (s32[]{:T(128)}, s32[]{:T(128)}, s32[]{:T(128)}) fusion(bf16[512,512]{1,0:T(8,128)(2,1)S(1)} %get-tuple-element.21, s32[512]{0:T(512)S(1)} %shift_right_arithmetic.162, s32[16,512]{1,0:T(8,128)S(1)} %and.71, bf16[512,512]{1,0:T(8,128)(2,1)S(1)} %get-tuple-element.25, f32[512,512]{1,0:T(8,128)S(1)} %get-tuple-element.23, f32[]{:T(128)} %bitcast.4), kind=kLoop, calls=%fused_computation.46 | loop fusion | flops 4718589 | bytes 2131984 | tf_op jit(solution)/shard_map/reduce_sum | solution.py:93
  49.7 1.5 %convert_multiply_fusion.1 = (f32[512,512]{1,0:T(8,128)}, f32[512,512]{1,0:T(8,128)S(1)}) fusion(bf16[512,512]{1,0:T(8,128)(2,1)S(1)} %fusion.6, f32[]{:T(128)} %bitcast.4, f32[512,512]{1,0:T(8,128)S(1)} %convolution_add_fusion.2, bf16[512,512]{1,0:T(8,128)(2,1)S(1)} %get-tuple-element.25), kind=kOutput, calls=%fused_computation.49 | convolution fusion | flops 269746176 | bytes 4194308 | tf_op jit(solution)/shard_map/dot_general | solution.py:66
  51.2 1.4 %convert_reduce_fusion.5 = (s32[]{:T(128)}, s32[]{:T(128)}, s32[]{:T(128)}) fusion(bf16[512,512]{1,0:T(8,128)(2,1)S(1)} %get-tuple-element.17, bf16[512,512]{1,0:T(8,128)(2,1)S(1)} %fusion.7, bf16[512,512]{1,0:T(8,128)(2,1)S(1)} %fusion.6, f32[512,512]{1,0:T(8,128)S(1)} %get-tuple-element.27, f32[]{:T(128)} %bitcast.4), kind=kLoop, calls=%fused_computation.47 | loop fusion | flops 2883581 | bytes 2621456 | tf_op jit(solution)/shard_map/reduce_sum | solution.py:92
  62.1 47.3 %psum.7 = s32[3]{0:T(128)} all-reduce(s32[3]{0:T(128)S(1)} %pad_add_fusion.3), channel_id=1, replica_groups=mesh['rows'=32] {'rows'}, use_global_device_ids=true, to_apply=%region_12.13 | all-reduce | flops 3 | bytes 24 | tf_op jit(solution)/shard_map/psum | solution.py:112
  109.4 2.8 %pad_maximum_fusion = f32[512,1024]{1,0:T(8,128)} fusion(f32[512,512]{1,0:T(8,128)} %get-tuple-element.22, f32[512,512]{1,0:T(8,128)S(1)} %copy-done.2), kind=kLoop, calls=%fused_computation | loop fusion | flops 524288 | bytes 4194304 | tf_op jit(solution)/shard_map/concatenate | solution.py:113
  (42 shorter events, 5.7 us)
Async XLA Ops:
  0.6 1.4 %copy-start.4 = (s32[16,512]{1,0:T(8,128)S(1)}, s32[16,512]{1,0:T(8,128)}, u32[]{:S(2)}) copy-start(s32[16,512]{1,0:T(8,128)} %param.6) | copy-start | bytes 98308
  0.6 1.4 %copy-start.5 = (s32[16,512]{1,0:T(8,128)S(1)}, s32[16,512]{1,0:T(8,128)}, u32[]{:S(2)}) copy-start(s32[16,512]{1,0:T(8,128)} %param.8) | copy-start | bytes 98308
  3.5 3.5 %collective-permute-start.1 = (s32[8,512]{1,0:T(8,128)S(1)}, s32[8,512]{1,0:T(8,128)S(1)}, u32[]{:S(2)}, u32[]{:S(2)}) collective-permute-start(s32[8,512]{1,0:T(8,128)S(1)} %fusion.25), channel_id=1, source_target_pairs={{0,31},{1,0},{2,1},{3,2},{4,3},{5,4},{6,5},{7,6},{8,7},{9,8},{10,9... | collective-permute-start | bytes 49160 | tf_op jit(solution)/shard_map/ppermute | solution.py:11
  4.8 9.8 %collective-permute-start = (s32[16,512]{1,0:T(8,128)S(1)}, s32[16,512]{1,0:T(8,128)S(1)}, u32[]{:S(2)}, u32[]{:S(2)}) collective-permute-start(s32[16,512]{1,0:T(8,128)S(1)} %get-tuple-element.9), channel_id=1, source_target_pairs={{0,1},{1,2},{2,3},{3,4},{4,5},{5,6},{6,7},{7,8},{8,9},{9,10},{10,1... | collective-permute-start | bytes 98312 | tf_op jit(solution)/shard_map/ppermute | solution.py:11
  13.8 5.3 %collective-permute-start.4 = (s32[16,512]{1,0:T(8,128)S(1)}, s32[16,512]{1,0:T(8,128)S(1)}, u32[]{:S(2)}, u32[]{:S(2)}) collective-permute-start(s32[16,512]{1,0:T(8,128)S(1)} %get-tuple-element.20), channel_id=1, source_target_pairs={{0,1},{1,2},{2,3},{3,4},{4,5},{5,6},{6,7},{7,8},{8,9},{9,10},{10,1... | collective-permute-start | bytes 98312 | tf_op jit(solution)/shard_map/ppermute | solution.py:11
  17.1 6.4 %collective-permute-start.2 = (s32[8,512]{1,0:T(8,128)S(1)}, s32[8,512]{1,0:T(8,128)S(1)}, u32[]{:S(2)}, u32[]{:S(2)}) collective-permute-start(s32[8,512]{1,0:T(8,128)S(1)} %fusion.24), channel_id=1, source_target_pairs={{0,31},{1,0},{2,1},{3,2},{4,3},{5,4},{6,5},{7,6},{8,7},{9,8},{10,9... | collective-permute-start | bytes 49160 | tf_op jit(solution)/shard_map/ppermute | solution.py:11
  21.6 2.0 %collective-permute-start.5 = (s32[8,512]{1,0:T(8,128)S(1)}, s32[8,512]{1,0:T(8,128)S(1)}, u32[]{:S(2)}, u32[]{:S(2)}) collective-permute-start(s32[8,512]{1,0:T(8,128)S(1)} %fusion.23), channel_id=1, source_target_pairs={{0,31},{1,0},{2,1},{3,2},{4,3},{5,4},{6,5},{7,6},{8,7},{9,8},{10,9... | collective-permute-start | bytes 49160 | tf_op jit(solution)/shard_map/ppermute | solution.py:11
  25.0 5.0 %copy-start.1 = (s32[256,512]{1,0:T(8,128)}, s32[256,512]{1,0:T(8,128)S(1)}, u32[]{:S(2)}) copy-start(s32[256,512]{1,0:T(8,128)S(1)} %get-tuple-element.19) | copy-start | bytes 1572868
  34.9 13.8 %collective-permute-start.3 = (s32[16,512]{1,0:T(8,128)S(1)}, s32[16,512]{1,0:T(8,128)S(1)}, u32[]{:S(2)}, u32[]{:S(2)}) collective-permute-start(s32[16,512]{1,0:T(8,128)S(1)} %get-tuple-element.24), channel_id=1, source_target_pairs={{0,1},{1,2},{2,3},{3,4},{4,5},{5,6},{6,7},{7,8},{8,9},{9,10},{10,1... | collective-permute-start | bytes 98312 | tf_op jit(solution)/shard_map/ppermute | solution.py:11
  44.4 1.0 copy-start
  44.4 1.4 %copy-start.3 = (s32[512,512]{0,1:T(8,128)S(1)}, s32[512,512]{0,1:T(8,128)}, u32[]{:S(2)}) copy-start(s32[512,512]{0,1:T(8,128)} %copy.13) | copy-start | bytes 3145732
  51.2 58.2 %copy-start.2 = (f32[512,512]{1,0:T(8,128)S(1)}, f32[512,512]{1,0:T(8,128)}, u32[]{:S(2)}) copy-start(f32[512,512]{1,0:T(8,128)} %get-tuple-element.26) | copy-start | bytes 3145732
where the time goes:
time: 113 us; the launch traced here: 112 us
  blocking collectives  47.3 us (42%)
  local copies, waits for them, and re-layouts  20.3 us (18%)
  matrix products  14.6 us (13%)
  other arithmetic  13.6 us (12%)
  between operations  11 us (10%)
  starting transfers between devices  5.31 us (5%)
    psum x1, blocking collectives, on_device(): stacked = lax.psum(stacked, 'rows')  47.3 us
    rev x3, local copies, waits for them, and re-layouts, unfold_within(): jnp.where(col_ids < row_ids, folded, jnp.zeros_like(folded))[::-1, ::-1]  8.41 us
    concatenate x3, local copies, waits for them, and re-layouts, unfold_within(): upper_half = jnp.concatenate([top_rows, bottom_rows], axis=0)  7.69 us
    dot_general x3, matrix products, support_across(): jnp.dot(across, next_within, preferred_element_type=jnp.float32)  6.13 us
    ppermute x6, starting transfers between devices, shifted(): lax.ppermute(array, axis, [(i, (i + by) % count) for i in range(count)])  5.31 us
    concatenate x3, other arithmetic, unfold_within(): upper_half = jnp.concatenate([top_rows, bottom_rows], axis=0)  4.27 us
    dot_general x3, matrix products, support_across(): between = jnp.dot(within, across, preferred_element_type=jnp.float32)  3.25 us
    concatenate x1, other arithmetic, on_device(): jnp.concatenate([inside * within.astype(jnp.float32), between * across.as...  2.76 us
  transfers between devices with their start and end apart: 6, of which 0 were waited for; matrix products, arithmetic and copies ran while one was open for 24% of the time, Pallas kernels for 0%

commit v1 on v0

--- a/solution.py
+++ b/solution.py
@@ -4,6 +4,15 @@
 from jax.sharding import PartitionSpec as P
 
 ITERS = 3
+
+
+def added_up(x, axis):
+    count = lax.axis_size(axis)
+    total, far = (x, 1)
+    while far < count:
+        total = total + lax.ppermute(total, axis, [(i, i ^ far) for i in range(count)])
+        far = 2 * far
+    return total
 
 
 def shifted(array, axis, by):
@@ -109,7 +118,7 @@
         counts.append(tally(within, new_within, across, new_across))
         within, across = (new_within, new_across)
     stacked = jnp.stack(counts)
-    stacked = lax.psum(stacked, "rows")
+    stacked = added_up(stacked, "rows")
     support = jnp.concatenate(
         [inside * within.astype(jnp.float32), between * across.astype(jnp.float32)], axis=1
     )

time: 113 us -> 89 us (0.79)
  the two profiles are of different devices: /device:TPU:12 before, /device:TPU:0 now
where the time goes in v1:
time: 89 us; the launch traced here: 88 us
  local copies, waits for them, and re-layouts  20.4 us (23%)
  matrix products  14.6 us (16%)
  other arithmetic  14.2 us (16%)
  starting transfers between devices  13.9 us (16%)
  waiting for transfers between devices  13.9 us (16%)
  between operations  11.1 us (12%)
    ppermute x5, waiting for transfers between devices, added_up(): lax.ppermute(total, axis, [(i, i ^ far) for i in range(count)])  13.8 us
    ppermute x6, starting transfers between devices, shifted(): lax.ppermute(array, axis, [(i, (i + by) % count) for i in range(count)])  12.5 us
    rev x3, local copies, waits for them, and re-layouts, unfold_within(): jnp.where(col_ids < row_ids, folded, jnp.zeros_like(folded))[::-1, ::-1]  8.42 us
    concatenate x3, local copies, waits for them, and re-layouts, unfold_within(): upper_half = jnp.concatenate([top_rows, bottom_rows], axis=0)  7.69 us
    dot_general x3, matrix products, support_across(): jnp.dot(across, next_within, preferred_element_type=jnp.float32)  6.13 us
    concatenate x3, other arithmetic, unfold_within(): upper_half = jnp.concatenate([top_rows, bottom_rows], axis=0)  4.27 us
    dot_general x3, matrix products, support_across(): between = jnp.dot(within, across, preferred_element_type=jnp.float32)  3.25 us
    concatenate x1, other arithmetic, on_device(): jnp.concatenate([inside * within.astype(jnp.float32), between * across.as...  2.76 us
  transfers between devices with their start and end apart: 11, of which 4 were waited for; matrix products, arithmetic and copies ran while one was open for 34% of the time, Pallas kernels for 0%

profile of v1, /device:TPU:0, one launch (start us, length us, event | category | flops | bytes accessed | tf_op | source)
XLA Modules:
  0.0 88.0 jit_solution(7774666239345363172)
XLA Ops:
  0.7 0.8 and.74
  2.4 0.9 %rev.18 = bf16[256,512]{1,0:T(8,128)(2,1)S(1)} reverse(bf16[256,512]{1,0:T(8,128)(2,1)S(1)} %slice.25), dimensions={0,1} | reverse | bytes 524288 | tf_op jit(solution)/shard_map/rev | solution.py:53
  3.5 6.5 %collective-permute-start.1 = (s32[8,512]{1,0:T(8,128)S(1)}, s32[8,512]{1,0:T(8,128)S(1)}, u32[]{:S(2)}, u32[]{:S(2)}) collective-permute-start(s32[8,512]{1,0:T(8,128)S(1)} %fusion.25), channel_id=1, source_target_pairs={{0,31},{1,0},{2,1},{3,2},{4,3},{5,4},{6,5},{7,6},{8,7},{9,8},{10,9... | collective-permute-start | bytes 49160 | tf_op jit(solution)/shard_map/ppermute | solution.py:20
  10.4 1.4 %fusion.47 = f32[512,512]{1,0:T(8,128)} fusion(bf16[512,512]{1,0:T(8,128)(2,1)S(1)} %get-tuple-element.17, bf16[512,512]{1,0:T(8,128)(2,1)S(1)} %get-tuple-element.16), kind=kOutput, calls=%fused_computation.93 | convolution fusion | flops 268435456 | bytes 2097152 | tf_op jit(solution)/shard_map/dot_general | solution.py:81
  12.7 0.8 rev.19
  13.5 1.1 %pad_add_fusion = s32[512,512]{1,0:T(8,128)} fusion(s32[256,512]{1,0:T(8,128)S(1)} %rev.19, s32[256,512]{1,0:T(8,128)S(1)} %get-tuple-element.14), kind=kLoop, calls=%fused_computation.21 | loop fusion | flops 262144 | bytes 2097152 | tf_op jit(solution)/shard_map/concatenate | solution.py:66
  14.5 2.6 %copy.8 = s32[512,512]{0,1:T(8,128)} copy(s32[512,512]{1,0:T(8,128)} %pad_add_fusion) | data formatting | bytes 2097152 | tf_op jit(solution)/shard_map/concatenate | solution.py:66
  17.1 2.2 %fusion.8 = (s32[16,512]{1,0:T(8,128)S(1)}, bf16[512,512]{1,0:T(8,128)(2,1)S(1)}) fusion(bf16[512,512]{1,0:T(8,128)(2,1)S(1)} %get-tuple-element.16, f32[]{:T(128)} %bitcast.4, f32[512,512]{1,0:T(8,128)} %fusion.47, s32[512,512]{0,1:T(8,128)} %copy.8, s32[256,512]{1,0:T(8,128)S(1)} %rev.19, s32[256,512]{1,0:T(8,128)S(1)} %get-tuple-element.14), kind=kOutput, calls=%fused_computation.25 | convolution fusion | flops 270786560 | bytes 4227076 | tf_op jit(solution)/shard_map/dot_general | solution.py:82
  20.9 0.9 %rev.20 = bf16[256,512]{1,0:T(8,128)(2,1)S(1)} reverse(bf16[256,512]{1,0:T(8,128)(2,1)S(1)} %slice.27), dimensions={0,1} | reverse | bytes 524288 | tf_op jit(solution)/shard_map/rev | solution.py:53
  22.0 5.4 %collective-permute-start.2 = (s32[8,512]{1,0:T(8,128)S(1)}, s32[8,512]{1,0:T(8,128)S(1)}, u32[]{:S(2)}, u32[]{:S(2)}) collective-permute-start(s32[8,512]{1,0:T(8,128)S(1)} %fusion.24), channel_id=1, source_target_pairs={{0,31},{1,0},{2,1},{3,2},{4,3},{5,4},{6,5},{7,6},{8,7},{9,8},{10,9... | collective-permute-start | bytes 49160 | tf_op jit(solution)/shard_map/ppermute | solution.py:20
  28.8 0.9 %rev.22 = bf16[256,512]{1,0:T(8,128)(2,1)S(1)} reverse(bf16[256,512]{1,0:T(8,128)(2,1)S(1)} %slice.29), dimensions={0,1} | reverse | bytes 524288 | tf_op jit(solution)/shard_map/rev | solution.py:53
  29.8 0.5 collective-permute-start.5
  30.4 1.4 %fusion.48 = f32[512,512]{1,0:T(8,128)} fusion(bf16[512,512]{1,0:T(8,128)(2,1)S(1)} %fusion.7, bf16[512,512]{1,0:T(8,128)(2,1)S(1)} %get-tuple-element.21), kind=kOutput, calls=%fused_computation.94 | convolution fusion | flops 268435456 | bytes 2097152 | tf_op jit(solution)/shard_map/dot_general | solution.py:81
  31.8 1.4 %fusion.28 = (s32[256,512]{1,0:T(8,128)}, s32[256,512]{1,0:T(8,128)}, s32[256,512]{1,0:T(8,128)}, s32[256,512]{1,0:T(8,128)S(1)}) fusion(s32[8,512]{1,0:T(8,128)S(1)} %collective-permute-done.5, s32[256]{0:T(256)S(1)} %shift_left.64, s32[8,512]{1,0:T(8,128)S(1)} %collective-permute-done.2), kind=kLoop, calls=%fused_computation.69 | loop fusion | flops 1310720 | bytes 2130944 | tf_op jit(solution)/shard_map/jit(_where)/select_n | solution.py:64
  33.2 3.9 %rev.21 = s32[256,512]{1,0:T(8,128)S(1)} reverse(s32[256,512]{1,0:T(8,128)} %get-tuple-element.18), dimensions={0,1} | reverse | bytes 1048576 | tf_op jit(solution)/shard_map/rev | solution.py:65
  37.1 1.1 %pad_add_fusion.1 = s32[512,512]{1,0:T(8,128)} fusion(s32[256,512]{1,0:T(8,128)S(1)} %rev.21, s32[256,512]{1,0:T(8,128)S(1)} %get-tuple-element.19), kind=kLoop, calls=%fused_computation.22 | loop fusion | flops 262144 | bytes 2097152 | tf_op jit(solution)/shard_map/concatenate | solution.py:66
  38.2 2.6 %copy.9 = s32[512,512]{0,1:T(8,128)} copy(s32[512,512]{1,0:T(8,128)} %pad_add_fusion.1) | data formatting | bytes 2097152 | tf_op jit(solution)/shard_map/concatenate | solution.py:66
  40.7 2.4 %fusion.9 = (s32[16,512]{1,0:T(8,128)S(1)}, bf16[512,512]{1,0:T(8,128)(2,1)S(1)}) fusion(bf16[512,512]{1,0:T(8,128)(2,1)S(1)} %get-tuple-element.21, f32[]{:T(128)} %bitcast.4, f32[512,512]{1,0:T(8,128)} %fusion.48, s32[512,512]{0,1:T(8,128)} %copy.9, s32[256,512]{1,0:T(8,128)S(1)} %rev.21, s32[256,512]{1,0:T(8,128)} %copy-done.1), kind=kOutput, calls=%fused_computation.27 | convolution fusion | flops 270786560 | bytes 4227076 | tf_op jit(solution)/shard_map/dot_general | solution.py:82
  43.2 3.8 %rev.23 = s32[256,512]{1,0:T(8,128)S(1)} reverse(s32[256,512]{1,0:T(8,128)} %get-tuple-element.11), dimensions={0,1} | reverse | bytes 1048576 | tf_op jit(solution)/shard_map/rev | solution.py:65
  47.0 2.1 %pad_add_fusion.2 = s32[512,512]{1,0:T(8,128)} fusion(s32[256,512]{1,0:T(8,128)S(1)} %rev.23, s32[256,512]{1,0:T(8,128)} %get-tuple-element.10), kind=kLoop, calls=%fused_computation.23 | loop fusion | flops 262144 | bytes 2097152 | tf_op jit(solution)/shard_map/concatenate | solution.py:66
  49.1 2.5 %copy.13 = s32[512,512]{0,1:T(8,128)} copy(s32[512,512]{1,0:T(8,128)} %pad_add_fusion.2) | data formatting | bytes 2097152 | tf_op jit(solution)/shard_map/concatenate | solution.py:66
  52.1 0.6 copy-done
  53.0 1.5 %convert_multiply_fusion = (f32[512,512]{1,0:T(8,128)}, f32[512,512]{1,0:T(8,128)S(1)}) fusion(bf16[512,512]{1,0:T(8,128)(2,1)S(1)} %get-tuple-element.25, f32[]{:T(128)} %bitcast.4, f32[512,512]{1,0:T(8,128)S(1)} %fusion.49, s32[512,512]{0,1:T(8,128)S(1)} %copy-done.3, s32[256,512]{1,0:T(8,128)S(1)} %rev.23, s32[256,512]{1,0:T(8,128)S(1)} %copy-done), kind=kOutput, calls=%fused_computation.48 | convolution fusion | flops 270532608 | bytes 5767172 | tf_op jit(solution)/shard_map/dot_general | solution.py:82
  54.5 1.5 %convert_reduce_fusion.4 = (s32[]{:T(128)}, s32[]{:T(128)}, s32[]{:T(128)}) fusion(bf16[512,512]{1,0:T(8,128)(2,1)S(1)} %get-tuple-element.21, s32[512]{0:T(512)S(1)} %shift_right_arithmetic.162, s32[16,512]{1,0:T(8,128)S(1)} %and.71, bf16[512,512]{1,0:T(8,128)(2,1)S(1)} %get-tuple-element.25, f32[512,512]{1,0:T(8,128)S(1)} %get-tuple-element.23, f32[]{:T(128)} %bitcast.4), kind=kLoop, calls=%fused_computation.46 | loop fusion | flops 4718589 | bytes 2131984 | tf_op jit(solution)/shard_map/reduce_sum | solution.py:102
  57.0 1.5 %convert_multiply_fusion.1 = (f32[512,512]{1,0:T(8,128)}, f32[512,512]{1,0:T(8,128)S(1)}) fusion(bf16[512,512]{1,0:T(8,128)(2,1)S(1)} %fusion.6, f32[]{:T(128)} %bitcast.4, f32[512,512]{1,0:T(8,128)S(1)} %convolution_add_fusion.2, bf16[512,512]{1,0:T(8,128)(2,1)S(1)} %get-tuple-element.25), kind=kOutput, calls=%fused_computation.49 | convolution fusion | flops 269746176 | bytes 4194308 | tf_op jit(solution)/shard_map/dot_general | solution.py:75
  58.4 1.4 %convert_reduce_fusion.5 = (s32[]{:T(128)}, s32[]{:T(128)}, s32[]{:T(128)}) fusion(bf16[512,512]{1,0:T(8,128)(2,1)S(1)} %get-tuple-element.17, bf16[512,512]{1,0:T(8,128)(2,1)S(1)} %fusion.7, bf16[512,512]{1,0:T(8,128)(2,1)S(1)} %fusion.6, f32[512,512]{1,0:T(8,128)S(1)} %get-tuple-element.27, f32[]{:T(128)} %bitcast.4), kind=kLoop, calls=%fused_computation.47 | loop fusion | flops 2883581 | bytes 2621456 | tf_op jit(solution)/shard_map/reduce_sum | solution.py:101
  69.4 2.8 %pad_maximum_fusion = f32[512,1024]{1,0:T(8,128)} fusion(f32[512,512]{1,0:T(8,128)} %get-tuple-element.22, f32[512,512]{1,0:T(8,128)S(1)} %copy-done.2), kind=kLoop, calls=%fused_computation | loop fusion | flops 524288 | bytes 4194304 | tf_op jit(solution)/shard_map/concatenate | solution.py:122
  72.2 3.6 %collective-permute-done.7 = s32[3]{0:T(128)S(1)} collective-permute-done((s32[3]{0:T(128)S(1)}, s32[3]{0:T(128)S(1)}, u32[]{:S(2)}, u32[]{:S(2)}) %collective-permute-start.7) | collective-permute-done | bytes 44 | tf_op jit(solution)/shard_map/ppermute | solution.py:13
  75.9 3.6 %collective-permute-done.8 = s32[3]{0:T(128)S(1)} collective-permute-done((s32[3]{0:T(128)S(1)}, s32[3]{0:T(128)S(1)}, u32[]{:S(2)}, u32[]{:S(2)}) %collective-permute-start.8) | collective-permute-done | bytes 44 | tf_op jit(solution)/shard_map/ppermute | solution.py:13
  79.4 3.6 %collective-permute-done.9 = s32[3]{0:T(128)S(1)} collective-permute-done((s32[3]{0:T(128)S(1)}, s32[3]{0:T(128)S(1)}, u32[]{:S(2)}, u32[]{:S(2)}) %collective-permute-start.9) | collective-permute-done | bytes 44 | tf_op jit(solution)/shard_map/ppermute | solution.py:13
  83.0 1.3 %collective-permute-start.10 = (s32[3]{0:T(128)S(1)}, s32[3]{0:T(128)S(1)}, u32[]{:S(2)}, u32[]{:S(2)}) collective-permute-start(s32[3]{0:T(128)S(1)} %add.87), channel_id=1, source_target_pairs={{0,16},{1,17},{2,18},{3,19},{4,20},{5,21},{6,22},{7,23},{8,24},{9,... | collective-permute-start | bytes 44 | tf_op jit(solution)/shard_map/ppermute | solution.py:13
  84.3 3.2 %collective-permute-done.10 = s32[3]{0:T(128)S(1)} collective-permute-done((s32[3]{0:T(128)S(1)}, s32[3]{0:T(128)S(1)}, u32[]{:S(2)}, u32[]{:S(2)}) %collective-permute-start.10) | collective-permute-done | bytes 44 | tf_op jit(solution)/shard_map/ppermute | solution.py:13
  (56 shorter events, 7.5 us)
Async XLA Ops:
  0.6 1.4 %copy-start.4 = (s32[16,512]{1,0:T(8,128)S(1)}, s32[16,512]{1,0:T(8,128)}, u32[]{:S(2)}) copy-start(s32[16,512]{1,0:T(8,128)} %param.6) | copy-start | bytes 98308
  0.6 1.4 %copy-start.5 = (s32[16,512]{1,0:T(8,128)S(1)}, s32[16,512]{1,0:T(8,128)}, u32[]{:S(2)}) copy-start(s32[16,512]{1,0:T(8,128)} %param.8) | copy-start | bytes 98308
  3.5 9.1 %collective-permute-start.1 = (s32[8,512]{1,0:T(8,128)S(1)}, s32[8,512]{1,0:T(8,128)S(1)}, u32[]{:S(2)}, u32[]{:S(2)}) collective-permute-start(s32[8,512]{1,0:T(8,128)S(1)} %fusion.25), channel_id=1, source_target_pairs={{0,31},{1,0},{2,1},{3,2},{4,3},{5,4},{6,5},{7,6},{8,7},{9,8},{10,9... | collective-permute-start | bytes 49160 | tf_op jit(solution)/shard_map/ppermute | solution.py:20
  10.3 9.1 %collective-permute-start = (s32[16,512]{1,0:T(8,128)S(1)}, s32[16,512]{1,0:T(8,128)S(1)}, u32[]{:S(2)}, u32[]{:S(2)}) collective-permute-start(s32[16,512]{1,0:T(8,128)S(1)} %get-tuple-element.9), channel_id=1, source_target_pairs={{0,1},{1,2},{2,3},{3,4},{4,5},{5,6},{6,7},{7,8},{8,9},{9,10},{10,1... | collective-permute-start | bytes 98312 | tf_op jit(solution)/shard_map/ppermute | solution.py:20
  19.4 8.0 %collective-permute-start.4 = (s32[16,512]{1,0:T(8,128)S(1)}, s32[16,512]{1,0:T(8,128)S(1)}, u32[]{:S(2)}, u32[]{:S(2)}) collective-permute-start(s32[16,512]{1,0:T(8,128)S(1)} %get-tuple-element.20), channel_id=1, source_target_pairs={{0,1},{1,2},{2,3},{3,4},{4,5},{5,6},{6,7},{7,8},{8,9},{9,10},{10,1... | collective-permute-start | bytes 98312 | tf_op jit(solution)/shard_map/ppermute | solution.py:20
  22.0 9.8 %collective-permute-start.2 = (s32[8,512]{1,0:T(8,128)S(1)}, s32[8,512]{1,0:T(8,128)S(1)}, u32[]{:S(2)}, u32[]{:S(2)}) collective-permute-start(s32[8,512]{1,0:T(8,128)S(1)} %fusion.24), channel_id=1, source_target_pairs={{0,31},{1,0},{2,1},{3,2},{4,3},{5,4},{6,5},{7,6},{8,7},{9,8},{10,9... | collective-permute-start | bytes 49160 | tf_op jit(solution)/shard_map/ppermute | solution.py:20
  29.8 2.0 %collective-permute-start.5 = (s32[8,512]{1,0:T(8,128)S(1)}, s32[8,512]{1,0:T(8,128)S(1)}, u32[]{:S(2)}, u32[]{:S(2)}) collective-permute-start(s32[8,512]{1,0:T(8,128)S(1)} %fusion.23), channel_id=1, source_target_pairs={{0,31},{1,0},{2,1},{3,2},{4,3},{5,4},{6,5},{7,6},{8,7},{9,8},{10,9... | collective-permute-start | bytes 49160 | tf_op jit(solution)/shard_map/ppermute | solution.py:20
  33.2 5.0 %copy-start.1 = (s32[256,512]{1,0:T(8,128)}, s32[256,512]{1,0:T(8,128)S(1)}, u32[]{:S(2)}) copy-start(s32[256,512]{1,0:T(8,128)S(1)} %get-tuple-element.19) | copy-start | bytes 1572868
  43.1 12.9 %collective-permute-start.3 = (s32[16,512]{1,0:T(8,128)S(1)}, s32[16,512]{1,0:T(8,128)S(1)}, u32[]{:S(2)}, u32[]{:S(2)}) collective-permute-start(s32[16,512]{1,0:T(8,128)S(1)} %get-tuple-element.24), channel_id=1, source_target_pairs={{0,1},{1,2},{2,3},{3,4},{4,5},{5,6},{6,7},{7,8},{8,9},{9,10},{10,1... | collective-permute-start | bytes 98312 | tf_op jit(solution)/shard_map/ppermute | solution.py:20
  51.6 1.0 %copy-start = (s32[256,512]{1,0:T(8,128)S(1)}, s32[256,512]{1,0:T(8,128)}, u32[]{:S(2)}) copy-start(s32[256,512]{1,0:T(8,128)} %get-tuple-element.10) | copy-start | bytes 1572868
  51.6 1.4 %copy-start.3 = (s32[512,512]{0,1:T(8,128)S(1)}, s32[512,512]{0,1:T(8,128)}, u32[]{:S(2)}) copy-start(s32[512,512]{0,1:T(8,128)} %copy.13) | copy-start | bytes 3145732
  58.4 10.9 %copy-start.2 = (f32[512,512]{1,0:T(8,128)S(1)}, f32[512,512]{1,0:T(8,128)}, u32[]{:S(2)}) copy-start(f32[512,512]{1,0:T(8,128)} %get-tuple-element.26) | copy-start | bytes 3145732
  69.3 2.8 %collective-permute-start.6 = (s32[3]{0:T(128)S(1)}, s32[3]{0:T(128)S(1)}, u32[]{:S(2)}, u32[]{:S(2)}) collective-permute-start(s32[3]{0:T(128)S(1)} %pad_add_fusion.3), channel_id=1, source_target_pairs={{0,1},{1,0},{2,3},{3,2},{4,5},{5,4},{6,7},{7,6},{8,9},{9,8},{10,11... | collective-permute-start | bytes 44 | tf_op jit(solution)/shard_map/ppermute | solution.py:13
  72.2 3.6 %collective-permute-start.7 = (s32[3]{0:T(128)S(1)}, s32[3]{0:T(128)S(1)}, u32[]{:S(2)}, u32[]{:S(2)}) collective-permute-start(s32[3]{0:T(128)S(1)} %fusion.71), channel_id=1, source_target_pairs={{0,2},{1,3},{2,0},{3,1},{4,6},{5,7},{6,4},{7,5},{8,10},{9,11},{10,... | collective-permute-start | bytes 44 | tf_op jit(solution)/shard_map/ppermute | solution.py:13
  75.9 3.6 %collective-permute-start.8 = (s32[3]{0:T(128)S(1)}, s32[3]{0:T(128)S(1)}, u32[]{:S(2)}, u32[]{:S(2)}) collective-permute-start(s32[3]{0:T(128)S(1)} %fusion.72), channel_id=1, source_target_pairs={{0,4},{1,5},{2,6},{3,7},{4,0},{5,1},{6,2},{7,3},{8,12},{9,13},{10,... | collective-permute-start | bytes 44 | tf_op jit(solution)/shard_map/ppermute | solution.py:13
  79.4 3.6 %collective-permute-start.9 = (s32[3]{0:T(128)S(1)}, s32[3]{0:T(128)S(1)}, u32[]{:S(2)}, u32[]{:S(2)}) collective-permute-start(s32[3]{0:T(128)S(1)} %add.86), channel_id=1, source_target_pairs={{0,8},{1,9},{2,10},{3,11},{4,12},{5,13},{6,14},{7,15},{8,0},{9,1},... | collective-permute-start | bytes 44 | tf_op jit(solution)/shard_map/ppermute | solution.py:13
  83.0 4.5 %collective-permute-start.10 = (s32[3]{0:T(128)S(1)}, s32[3]{0:T(128)S(1)}, u32[]{:S(2)}, u32[]{:S(2)}) collective-permute-start(s32[3]{0:T(128)S(1)} %add.87), channel_id=1, source_target_pairs={{0,16},{1,17},{2,18},{3,19},{4,20},{5,21},{6,22},{7,23},{8,24},{9,... | collective-permute-start | bytes 44 | tf_op jit(solution)/shard_map/ppermute | solution.py:13
